TPU v7x, 512 devices: a whole 4x4x16 slice. The times are simulated.
512 devices in a mesh: ctx: 64 (over x_lo, z, core), tp: 8 (over y, x_hi).
Axes of the slice: x: 4 (x_hi: 2, x_lo: 2; x = x_hi * 2 + x_lo), y: 4, z: 16, core: 2. Of those that a mesh axis runs over, the one named last changes fastest.
Arguments:
- queries: bfloat16 [16384, 12288], P(('ctx', 'tp')), may hold values from -64 to 64
- keys: bfloat16 [16384, 1024], P(('ctx', 'tp')), may hold values from -4 to 4
- values: bfloat16 [16384, 1024], P(('ctx', 'tp')), may hold values from -6 to 6
- block_order: int32 [64], replicated, may hold values from 0 to 63, each once
Outputs:
- attended: bfloat16 [16384, 12288], P(('ctx', 'tp'))
Inputs may be any that keep to these rules, and one draw needn't show every extreme that they name: A permutation: block r holds sequence span block_order[r] in its first 128 rows and span 2 * 64 - 1 - block_order[r] in its last 128 rows.
All inputs are finite; a program needn't handle non-finite values.
Results may differ from a plain program's by a relative error of at most 0.003.
Values may be sent and summed in bfloat16 or wider, within the bound.
A program may use at most 64 MiB of HBM per device.

v0:
```python
import math

import jax
import jax.numpy as jnp
from jax import lax
from jax.sharding import PartitionSpec as P

HD = 128
PREV = 3


MASKED_SCORE = -1e30


def passed_along(value, axis, steps):
    count = lax.axis_size(axis)
    pairs = [(source, (source + steps) % count) for source in range(count)]
    return lax.ppermute(value, axis, pairs)


def block_positions(block_order, block_index, first_row, count, span_rows):
    block_total = block_order.shape[0]
    leading = jnp.sum(
        jnp.where(jnp.arange(block_total, dtype=jnp.int32) == block_index, block_order, 0)
    )
    row_ids = first_row + jnp.arange(count, dtype=jnp.int32)
    return jnp.where(
        row_ids < span_rows,
        leading * span_rows + row_ids,
        (2 * block_total - 1 - leading) * span_rows + row_ids - span_rows,
    )


def update(carried, queries_h, query_pos, key_part, value_part, key_pos):
    piece_rows = key_part.shape[0]
    block_rows = math.gcd(piece_rows, 256)
    block_count = piece_rows // block_rows
    score_scale = 1.0 / math.sqrt(queries_h.shape[-1])
    key_blocks = key_part.reshape(block_count, block_rows, key_part.shape[1], key_part.shape[2])
    value_blocks = value_part.reshape(
        block_count, block_rows, value_part.shape[1], value_part.shape[2]
    )
    pos_blocks = key_pos.reshape(block_count, block_rows)

    def advance(running, blocks_in):
        running_max, running_sum, numerator = running
        key_block, value_block, pos_block = blocks_in
        scores = (
            jnp.einsum("tkgd,skd->tkgs", queries_h, key_block, preferred_element_type=jnp.float32)
            * score_scale
        )
        visible = pos_block[None, None, None, :] <= query_pos[:, None, None, None]
        block_max = jnp.max(jnp.where(visible, scores, MASKED_SCORE), axis=-1)
        new_max = jnp.maximum(running_max, block_max)
        exp_scores = jnp.where(visible, jnp.exp(scores - new_max[..., None]), 0.0)
        rescale = jnp.exp(running_max - new_max)
        running_sum = running_sum * rescale + jnp.sum(exp_scores, axis=-1)
        weights = exp_scores.astype(jnp.bfloat16)
        numerator = numerator * rescale[..., None] + jnp.einsum(
            "tkgs,skd->tkgd", weights, value_block, preferred_element_type=jnp.float32
        )
        return ((new_max, running_sum, numerator), None)

    final_state, _ = lax.scan(advance, carried, (key_blocks, value_blocks, pos_blocks))
    return final_state


def per_device(queries, keys, values, block_order):
    block_total = block_order.shape[0]
    ctx_index = lax.axis_index("ctx")
    local_q, local_k, local_v = (
        lax.all_to_all(queries, "tp", split_axis=1, concat_axis=0, tiled=True),
        lax.all_to_all(keys, "tp", split_axis=1, concat_axis=0, tiled=True),
        lax.all_to_all(values, "tp", split_axis=1, concat_axis=0, tiled=True),
    )
    first_row = 0
    token_rows = local_q.shape[0]
    block_rows = local_k.shape[0]
    span_rows = block_rows // 2
    kv_local = local_k.shape[1] // HD
    group_size = local_q.shape[1] // (HD * kv_local)
    queries_h = local_q.reshape(token_rows, kv_local, group_size, HD)
    query_pos = block_positions(block_order, ctx_index, first_row, token_rows, span_rows)
    own_pair = jnp.stack(
        [local_k.reshape(block_rows, kv_local, HD), local_v.reshape(block_rows, kv_local, HD)]
    )
    state = (
        jnp.full((token_rows, kv_local, group_size), MASKED_SCORE, jnp.float32),
        jnp.zeros((token_rows, kv_local, group_size), jnp.float32),
        jnp.zeros((token_rows, kv_local, group_size, HD), jnp.float32),
    )
    own_pos = block_positions(block_order, ctx_index, 0, block_rows, span_rows)
    state = update(state, queries_h, query_pos, own_pair[0], own_pair[1], own_pos)
    moving = own_pair
    for step in range(1, PREV + 1):
        moving = passed_along(moving, "ctx", 1)
        source = (ctx_index - step) % block_total
        source_pos = block_positions(block_order, source, 0, block_rows, span_rows)
        state = update(state, queries_h, query_pos, moving[0], moving[1], source_pos)
    running_max, running_sum, numerator = state
    attended = (numerator / running_sum[..., None]).astype(jnp.bfloat16)
    attended = attended.reshape(token_rows, kv_local * group_size * HD)
    attended = lax.all_to_all(attended, "tp", split_axis=0, concat_axis=1, tiled=True)
    return attended


def solution(mesh):
    return jax.shard_map(
        per_device,
        mesh=mesh,
        in_specs=(P(("ctx", "tp"), None), P(("ctx", "tp"), None), P(("ctx", "tp"), None), P()),
        out_specs=P(("ctx", "tp"), None),
        check_vma=False,
    )
```

profile of v0, /device:TPU:2, one launch (start us, length us, event | category | flops | bytes accessed | tf_op | source)
XLA Modules:
  0.0 91.5 jit_solution(4069063614172192647)
XLA Ops:
  0.0 0.0 copy-start
  0.0 0.8 copy-done
  0.8 0.6 copy_bitcast_fusion.2
  1.5 6.0 %all-to-all-start = ((bf16[32,8,128]{2,0,1:T(8,128)(2,1)}), bf16[32,8,128]{2,0,1:T(8,128)(2,1)S(1)}, u32[]{:S(2)}, u32[]{:S(2)}) async-start(bf16[32,8,128]{2,0,1:T(8,128)(2,1)} %copy_bitcast_fusion.2), calls=%async_computation | async-start | bytes 131072 | tf_op jit(solution)/shard_map/all_to_all | solution.py:73
  7.5 1.5 %copy_bitcast_fusion.1 = bf16[32,8,128]{2,0,1:T(8,128)(2,1)} fusion(bf16[32,1024]{1,0:T(8,128)(2,1)} %param.6), kind=kLoop, calls=%fused_computation.76 | loop fusion | bytes 131072 | tf_op jit(solution)/shard_map/all_to_all | solution.py:74
  9.0 6.4 %all-to-all-done = bf16[32,8,128]{2,0,1:T(8,128)(2,1)S(1)} async-done(((bf16[32,8,128]{2,0,1:T(8,128)(2,1)}), bf16[32,8,128]{2,0,1:T(8,128)(2,1)S(1)}, u32[]{:S(2)}, u32[]{:S(2)}) %all-to-all-start) | async-done | bytes 65568 | tf_op jit(solution)/shard_map/all_to_all | solution.py:73
  15.4 3.3 %all-to-all-start.2 = ((bf16[32,8,128]{2,0,1:T(8,128)(2,1)}), bf16[32,8,128]{2,0,1:T(8,128)(2,1)S(1)}, u32[]{:S(2)}, u32[]{:S(2)}) async-start(bf16[32,8,128]{2,0,1:T(8,128)(2,1)} %copy_bitcast_fusion.1), calls=%async_computation.2 | async-start | bytes 131072 | tf_op jit(solution)/shard_map/all_to_all | solution.py:74
  18.7 1.3 %fusion.72 = (s32[]{:T(128)}, s32[]{:T(128)}, s32[]{:T(128)}, s32[]{:T(128)}) fusion(s32[64]{0:T(128)} %param.7, s32[]{:T(128)S(6)} %select_n.94, s32[]{:T(128)S(6)} %select_n.84, s32[]{:T(128)S(6)} %axis_index.15, s32[]{:T(128)S(6)} %select_n.89), kind=kLoop, calls=%fused_computation.102 | loop fusion | flops 764 | bytes 288 | tf_op jit(solution)/shard_map/reduce_sum | solution.py:23
  21.4 2.1 %copy.90 = bf16[4,8,8,1536]{3,2,0,1:T(8,128)(2,1)} copy(bf16[4,8,8,1536]{3,2,1,0:T(8,128)(2,1)} %bitcast.208) | data formatting | bytes 1572864 | tf_op jit(solution)/shard_map/all_to_all | solution.py:72
  23.4 3.1 %all-to-all-done.2 = bf16[32,8,128]{2,0,1:T(8,128)(2,1)S(1)} async-done(((bf16[32,8,128]{2,0,1:T(8,128)(2,1)}), bf16[32,8,128]{2,0,1:T(8,128)(2,1)S(1)}, u32[]{:S(2)}, u32[]{:S(2)}) %all-to-all-start.2) | async-done | bytes 65568 | tf_op jit(solution)/shard_map/all_to_all | solution.py:74
  26.5 4.1 %all-to-all-start.1 = ((bf16[32,8,1536]{2,0,1:T(8,128)(2,1)}), bf16[32,8,1536]{2,0,1:T(8,128)(2,1)S(1)}, u32[]{:S(2)}, u32[]{:S(2)}) async-start(bf16[32,8,1536]{2,0,1:T(8,128)(2,1)} %bitcast.205), calls=%async_computation.1 | async-start | bytes 1572864 | tf_op jit(solution)/shard_map/all_to_all | solution.py:72
  33.1 1.9 %collective-permute-start = (bf16[2,256,1,128]{3,1,2,0:T(8,128)(2,1)S(1)}, bf16[2,256,1,128]{3,1,2,0:T(8,128)(2,1)S(1)}, u32[]{:S(2)}, u32[]{:S(2)}) collective-permute-start(bf16[2,256,1,128]{3,1,2,0:T(8,128)(2,1)S(1)} %pad_maximum_fusion), channel_id=1, source_target_pairs={{0,8},{8,16},{16,24},{24,32},{32,40},{40,48},{48,56},{56,64},{64,7... | collective-permute-start | bytes 393224 | tf_op jit(solution)/shard_map/ppermute | solution.py:18
  36.1 9.3 %collective-permute-done = bf16[2,256,1,128]{3,1,2,0:T(8,128)(2,1)S(1)} collective-permute-done((bf16[2,256,1,128]{3,1,2,0:T(8,128)(2,1)S(1)}, bf16[2,256,1,128]{3,1,2,0:T(8,128)(2,1)S(1)}, u32[]{:S(2)}, u32[]{:S(2)}) %collective-permute-start) | collective-permute-done | bytes 131104 | tf_op jit(solution)/shard_map/ppermute | solution.py:18
  45.4 1.9 %collective-permute-start.1 = (bf16[2,256,1,128]{3,1,2,0:T(8,128)(2,1)S(1)}, bf16[2,256,1,128]{3,1,2,0:T(8,128)(2,1)S(1)}, u32[]{:S(2)}, u32[]{:S(2)}) collective-permute-start(bf16[2,256,1,128]{3,1,2,0:T(8,128)(2,1)S(1)} %collective-permute-done), channel_id=1, source_target_pairs={{0,8},{8,16},{16,24},{24,32},{32,40},{40,48},{48,56},{56,64},{64,7... | collective-permute-start | bytes 393224 | tf_op jit(solution)/shard_map/ppermute | solution.py:18
  47.4 0.2 broadcast_compare_fusion.3
  47.6 6.2 %collective-permute-done.1 = bf16[2,256,1,128]{3,1,2,0:T(8,128)(2,1)S(1)} collective-permute-done((bf16[2,256,1,128]{3,1,2,0:T(8,128)(2,1)S(1)}, bf16[2,256,1,128]{3,1,2,0:T(8,128)(2,1)S(1)}, u32[]{:S(2)}, u32[]{:S(2)}) %collective-permute-start.1) | collective-permute-done | bytes 131104 | tf_op jit(solution)/shard_map/ppermute | solution.py:18
  53.8 1.9 %collective-permute-start.2 = (bf16[2,256,1,128]{3,1,2,0:T(8,128)(2,1)S(1)}, bf16[2,256,1,128]{3,1,2,0:T(8,128)(2,1)S(1)}, u32[]{:S(2)}, u32[]{:S(2)}) collective-permute-start(bf16[2,256,1,128]{3,1,2,0:T(8,128)(2,1)S(1)} %collective-permute-done.1), channel_id=1, source_target_pairs={{0,8},{8,16},{16,24},{24,32},{32,40},{40,48},{48,56},{56,64},{64,7... | collective-permute-start | bytes 393224 | tf_op jit(solution)/shard_map/ppermute | solution.py:18
  55.7 0.0 all-to-all-done.1
  55.8 0.5 reshape.398
  56.3 0.7 fusion.9
  57.0 0.7 fusion.6
  57.7 0.7 fusion.3
  58.5 3.7 %collective-permute-done.2 = bf16[2,256,1,128]{3,1,2,0:T(8,128)(2,1)S(1)} collective-permute-done((bf16[2,256,1,128]{3,1,2,0:T(8,128)(2,1)S(1)}, bf16[2,256,1,128]{3,1,2,0:T(8,128)(2,1)S(1)}, u32[]{:S(2)}, u32[]{:S(2)}) %collective-permute-start.2) | collective-permute-done | bytes 131104 | tf_op jit(solution)/shard_map/ppermute | solution.py:18
  62.2 0.7 fusion
  63.0 1.0 %fusion.30 = f32[256,12,128]{2,0,1:T(8,128)S(1)} fusion(bf16[256,128,1]{1,0,2:T(8,128)(2,1)S(1)} %bitcast.212, f32[256,256,12]{1,0,2:T(8,128)S(1)} %get-tuple-element.126, f32[256,12]{0,1:T(8,128)S(1)} %get-tuple-element.96, pred[256,256]{0,1:T(8,128)(4,1)S(1)} %get-tuple-element.97), kind=kOutput, calls=%fused_computation.35 | convolution fusion | flops 204472320 | bytes 4861952 | tf_op jit(solution)/shard_map/while/body/eval_jaxpr/tkgs,skd->tkgd/dot_general | solution.py:59
  64.0 1.3 %fusion.12 = (f32[256,12]{0,1:T(8,128)S(1)}, f32[256,12]{0,1:T(8,128)S(1)}) fusion(f32[256,256,12]{1,0,2:T(8,128)S(1)} %get-tuple-element.126, f32[256,12]{0,1:T(8,128)S(1)} %get-tuple-element.96, pred[256,256]{0,1:T(8,128)(4,1)S(1)} %get-tuple-element.97, f32[256,12]{0,1:T(8,128)S(1)} %get-tuple-element.94, f32[256,256,12]{1,0,2:T(8,128)S(1)} %get-tuple-element.115, ...), kind=kLoop, calls=%fused_computation.20 | loop fusion | flops 6285312 | bytes 6471680 | tf_op jit(solution)/shard_map/while/body/eval_jaxpr/reduce_sum | solution.py:57
  65.3 1.3 %fusion.16 = (f32[256,12]{0,1:T(8,128)S(1)}, f32[256,12]{0,1:T(8,128)S(1)}) fusion(f32[256,256,12]{1,0,2:T(8,128)S(1)} %get-tuple-element.113, f32[256,12]{0,1:T(8,128)S(1)} %get-tuple-element.93, pred[256,256]{0,1:T(8,128)(4,1)S(1)} %get-tuple-element.98, f32[256,12]{0,1:T(8,128)S(1)} %get-tuple-element.92, f32[256,256,12]{1,0,2:T(8,128)S(1)} %get-tuple-element.111, ...), kind=kLoop, calls=%fused_computation.24 | loop fusion | flops 6285312 | bytes 6471680 | tf_op jit(solution)/shard_map/while/body/eval_jaxpr/reduce_sum | solution.py:57
  66.7 1.0 %fusion.27 = f32[128,256,12]{0,1,2:T(8,128)S(1)} fusion(f32[256,256,12]{1,0,2:T(8,128)S(1)} %get-tuple-element.115, f32[256,12]{0,1:T(8,128)S(1)} %get-tuple-element.94, pred[256,256]{0,1:T(8,128)(4,1)S(1)} %get-tuple-element.109, bf16[2,256,1,128]{3,1,2,0:T(8,128)(2,1)S(1)} %collective-permute-done), kind=kOutput, calls=%fused_computation.33 | convolution fusion | flops 204472320 | bytes 4866048 | tf_op jit(solution)/shard_map/while/body/eval_jaxpr/tkgs,skd->tkgd/dot_general | solution.py:59
  67.7 1.0 %fusion.24 = f32[128,256,12]{0,1,2:T(8,128)S(1)} fusion(f32[256,256,12]{1,0,2:T(8,128)S(1)} %get-tuple-element.113, f32[256,12]{0,1:T(8,128)S(1)} %get-tuple-element.93, pred[256,256]{0,1:T(8,128)(4,1)S(1)} %get-tuple-element.98, bf16[2,256,1,128]{3,1,2,0:T(8,128)(2,1)S(1)} %collective-permute-done.1), kind=kOutput, calls=%fused_computation.31 | convolution fusion | flops 204472320 | bytes 4866048 | tf_op jit(solution)/shard_map/while/body/eval_jaxpr/tkgs,skd->tkgd/dot_general | solution.py:59
  68.6 3.2 %fusion.58 = bf16[256,1,12,128]{3,0,2,1:T(8,128)(2,1)S(1)} fusion(f32[256,256,12]{1,0,2:T(8,128)S(1)} %get-tuple-element.111, f32[256,12]{0,1:T(8,128)S(1)} %get-tuple-element.92, pred[256,256]{0,1:T(8,128)(4,1)S(1)} %get-tuple-element.108, f32[128,256,12]{0,1,2:T(8,128)S(1)} %fusion.24, f32[128,256,12]{0,1,2:T(8,128)S(1)} %fusion.27, ...), kind=kOutput, calls=%fused_computation.61 | convolution fusion | flops 208011264 | bytes 8880128 | tf_op jit(solution)/shard_map/while/body/eval_jaxpr/tkgs,skd->tkgd/dot_general | solution.py:59
  71.8 0.5 copy.52
  72.3 0.5 all_to_all.59
  72.9 17.7 %all_to_all.67 = bf16[8,32,1536]{2,1,0:T(8,128)(2,1)S(1)} all-to-all(bf16[8,32,1536]{2,1,0:T(8,128)(2,1)S(1)} %all_to_all.59), channel_id=1, replica_groups=mesh['ctx'=64,'tp'=8] {'tp'}, dimensions={0} | all-to-all | bytes 1572864 | tf_op jit(solution)/shard_map/all_to_all | solution.py:103
  90.6 0.9 %copy.70 = bf16[8,4,8,1536]{3,2,0,1:T(8,128)(2,1)} copy(bf16[8,4,8,1536]{3,2,1,0:T(8,128)(2,1)S(1)} %bitcast.207) | data formatting | bytes 1572864 | tf_op jit(solution)/shard_map/all_to_all | solution.py:103
  (7 shorter events, 0.1 us)
Async XLA Ops:
  0.0 0.8 copy-start
  1.5 13.9 %all-to-all-start = ((bf16[32,8,128]{2,0,1:T(8,128)(2,1)}), bf16[32,8,128]{2,0,1:T(8,128)(2,1)S(1)}, u32[]{:S(2)}, u32[]{:S(2)}) async-start(bf16[32,8,128]{2,0,1:T(8,128)(2,1)} %copy_bitcast_fusion.2), calls=%async_computation | async-start | bytes 131072 | tf_op jit(solution)/shard_map/all_to_all | solution.py:73
  15.4 11.1 %all-to-all-start.2 = ((bf16[32,8,128]{2,0,1:T(8,128)(2,1)}), bf16[32,8,128]{2,0,1:T(8,128)(2,1)S(1)}, u32[]{:S(2)}, u32[]{:S(2)}) async-start(bf16[32,8,128]{2,0,1:T(8,128)(2,1)} %copy_bitcast_fusion.1), calls=%async_computation.2 | async-start | bytes 131072 | tf_op jit(solution)/shard_map/all_to_all | solution.py:74
  26.5 29.2 %all-to-all-start.1 = ((bf16[32,8,1536]{2,0,1:T(8,128)(2,1)}), bf16[32,8,1536]{2,0,1:T(8,128)(2,1)S(1)}, u32[]{:S(2)}, u32[]{:S(2)}) async-start(bf16[32,8,1536]{2,0,1:T(8,128)(2,1)} %bitcast.205), calls=%async_computation.1 | async-start | bytes 1572864 | tf_op jit(solution)/shard_map/all_to_all | solution.py:72
  33.1 12.4 %collective-permute-start = (bf16[2,256,1,128]{3,1,2,0:T(8,128)(2,1)S(1)}, bf16[2,256,1,128]{3,1,2,0:T(8,128)(2,1)S(1)}, u32[]{:S(2)}, u32[]{:S(2)}) collective-permute-start(bf16[2,256,1,128]{3,1,2,0:T(8,128)(2,1)S(1)} %pad_maximum_fusion), channel_id=1, source_target_pairs={{0,8},{8,16},{16,24},{24,32},{32,40},{40,48},{48,56},{56,64},{64,7... | collective-permute-start | bytes 393224 | tf_op jit(solution)/shard_map/ppermute | solution.py:18
  45.4 8.4 %collective-permute-start.1 = (bf16[2,256,1,128]{3,1,2,0:T(8,128)(2,1)S(1)}, bf16[2,256,1,128]{3,1,2,0:T(8,128)(2,1)S(1)}, u32[]{:S(2)}, u32[]{:S(2)}) collective-permute-start(bf16[2,256,1,128]{3,1,2,0:T(8,128)(2,1)S(1)} %collective-permute-done), channel_id=1, source_target_pairs={{0,8},{8,16},{16,24},{24,32},{32,40},{40,48},{48,56},{56,64},{64,7... | collective-permute-start | bytes 393224 | tf_op jit(solution)/shard_map/ppermute | solution.py:18
  53.8 8.4 %collective-permute-start.2 = (bf16[2,256,1,128]{3,1,2,0:T(8,128)(2,1)S(1)}, bf16[2,256,1,128]{3,1,2,0:T(8,128)(2,1)S(1)}, u32[]{:S(2)}, u32[]{:S(2)}) collective-permute-start(bf16[2,256,1,128]{3,1,2,0:T(8,128)(2,1)S(1)} %collective-permute-done.1), channel_id=1, source_target_pairs={{0,8},{8,16},{16,24},{24,32},{32,40},{40,48},{48,56},{56,64},{64,7... | collective-permute-start | bytes 393224 | tf_op jit(solution)/shard_map/ppermute | solution.py:18
where the time goes:
time: 92.2 us; the launch traced here: 91.5 us
  waiting for transfers between devices  28.7 us (31%)
  starting transfers between devices  19.2 us (21%)
  blocking collectives  17.7 us (19%)
  matrix products  8.98 us (10%)
  local copies, waits for them, and re-layouts  7.58 us (8%)
  between operations  5.06 us (5%)
  other arithmetic  4.28 us (5%)
    ppermute x3, waiting for transfers between devices, passed_along(): return lax.ppermute(value, axis, pairs)  19.3 us
    all_to_all x1, blocking collectives, per_device(): lax.all_to_all(attended, 'tp', split_axis=0, concat_axis=1, tiled=True)  17.7 us
    all_to_all x1, waiting for transfers between devices, per_device(): lax.all_to_all(keys, 'tp', split_axis=1, concat_axis=0, tiled=True)  6.38 us
    dot_general x4, matrix products, advance(): jnp.einsum('tkgs,skd->tkgd', weights, value_block, preferred_element_type...  6.12 us
    all_to_all x1, starting transfers between devices, per_device(): lax.all_to_all(keys, 'tp', split_axis=1, concat_axis=0, tiled=True)  6.03 us
    ppermute x3, starting transfers between devices, passed_along(): return lax.ppermute(value, axis, pairs)  5.74 us
    all_to_all x1, starting transfers between devices, per_device(): lax.all_to_all(queries, 'tp', split_axis=1, concat_axis=0, tiled=True)  4.08 us
    all_to_all x1, starting transfers between devices, per_device(): lax.all_to_all(values, 'tp', split_axis=1, concat_axis=0, tiled=True)  3.35 us
  transfers between devices with their start and end apart: 6, of which 5 were waited for; matrix products, arithmetic and copies ran while one was open for 9% of the time, Pallas kernels for 0%

commit v1 on v0

v1 whole, which is shorter than its diff:
```python
import functools
import math

import jax
import jax.numpy as jnp
from jax import lax
from jax.experimental import pallas as pl
from jax.experimental.pallas import tpu as pltpu
from jax.sharding import PartitionSpec as P

HD = 128
PREV = 3
MASKED_SCORE = -1e30
MESH = pl.DeviceIdType.MESH
ORDER = ((0, 0), (2, 0), (2, 1), (1, 1), (3, 1), (0, 1), (1, 0), (3, 0))


def pick(index, values):
    total = jnp.int32(0)
    for position, value in enumerate(values):
        if value:
            total = total + jnp.where(index == position, jnp.int32(value), jnp.int32(0))
    return total


def kernel(
    blocks, q_hbm, k_hbm, v_hbm, order_ref, out_hbm,
    q_buf, kv_buf, k_vm, v_vm, vext, o_buf,
    local_sem, kv_ss, kv_rs, q_ss, q_rs, f_ss, f_rs, o_ss, o_rs,
):
    ctx = lax.axis_index("ctx")
    tp = lax.axis_index("tp")
    rows = q_hbm.shape[0]
    width = q_buf.shape[2]
    group = width // HD
    y, xh = lax.div(tp, 2), lax.rem(tp, 2)

    def slot_of(dy, dx):
        return lax.rem(y + dy, 4) * 2 + lax.rem(xh + dx, 2)

    def lanes(slot, size):
        return pl.ds(pl.multiple_of(slot * size, size), size)

    ahead = [lax.rem(ctx + step, blocks) for step in range(1, PREV + 1)]
    behind = [lax.rem(ctx + blocks - step, blocks) for step in range(1, PREV + 1)]

    k_load = pltpu.make_async_copy(k_hbm, k_vm, local_sem.at[0])
    v_load = pltpu.make_async_copy(v_hbm, v_vm, local_sem.at[1])
    own_k = pltpu.make_async_copy(k_hbm.at[:, lanes(tp, HD)], kv_buf.at[0, tp, 0], local_sem.at[2])
    own_v = pltpu.make_async_copy(v_hbm.at[:, lanes(tp, HD)], kv_buf.at[0, tp, 1], local_sem.at[3])
    own_q = pltpu.make_async_copy(q_hbm.at[:, lanes(tp, width)], q_buf.at[tp], local_sem.at[4])
    for copy in (k_load, v_load, own_k, own_v, own_q):
        copy.start()

    barrier = pltpu.get_barrier_semaphore()
    for dy, dx in ORDER[1:]:
        pl.semaphore_signal(barrier, inc=1, device_id=(ctx, slot_of(dy, dx)), device_id_type=MESH)
    for other in behind:
        pl.semaphore_signal(barrier, inc=1, device_id=(other, tp), device_id_type=MESH)
    pl.semaphore_wait(barrier, len(ORDER) - 1 + PREV)

    def kv_copy(part, source, origin, peer):
        return pltpu.make_async_remote_copy(
            src_ref=source.at[:, lanes(peer, HD)],
            dst_ref=kv_buf.at[0, origin, part],
            send_sem=kv_ss.at[peer, part],
            recv_sem=kv_rs.at[origin, part],
            device_id=(ctx, peer),
            device_id_type=MESH,
        )

    def q_copy(origin, peer):
        return pltpu.make_async_remote_copy(
            src_ref=q_hbm.at[:, lanes(peer, width)],
            dst_ref=q_buf.at[origin],
            send_sem=q_ss.at[peer],
            recv_sem=q_rs.at[origin],
            device_id=(ctx, peer),
            device_id_type=MESH,
        )

    def forward(slot, step):
        return pltpu.make_async_remote_copy(
            src_ref=kv_buf.at[0, slot],
            dst_ref=kv_buf.at[step, slot],
            send_sem=f_ss.at[slot, step - 1],
            recv_sem=f_rs.at[slot, step - 1],
            device_id=(ahead[step - 1], tp),
            device_id_type=MESH,
        )

    def o_copy(origin, peer):
        return pltpu.make_async_remote_copy(
            src_ref=o_buf.at[peer],
            dst_ref=out_hbm.at[:, lanes(origin, width)],
            send_sem=o_ss.at[peer],
            recv_sem=o_rs.at[origin],
            device_id=(ctx, peer),
            device_id_type=MESH,
        )

    k_load.wait()
    v_load.wait()
    for dy, dx in ORDER[1:]:
        kv_copy(0, k_vm, tp, slot_of(dy, dx)).start()
        kv_copy(1, v_vm, tp, slot_of(dy, dx)).start()
    for dy, dx in ORDER[1:]:
        q_copy(tp, slot_of(dy, dx)).start()

    own_k.wait()
    own_v.wait()
    for dy, dx in ((0, 0), (1, 0), (3, 0), (0, 1), (1, 1), (3, 1), (2, 0), (2, 1)):
        slot = slot_of(dy, dx)
        if (dy, dx) != (0, 0):
            kv_copy(0, k_vm, slot, slot).wait_recv()
            kv_copy(1, v_vm, slot, slot).wait_recv()
        for step in range(1, PREV + 1):
            forward(slot, step).start()

    vext[:, :, HD:] = jnp.ones(vext.shape[:2] + (HD,), jnp.bfloat16)
    vext[0, :, :HD] = kv_buf[0, :, 1].reshape(8 * rows, HD)
    for step in range(1, PREV + 1):
        for slot in range(8):
            forward(slot, step).wait_recv()
        vext[step, :, :HD] = kv_buf[step, :, 1].reshape(8 * rows, HD)
    own_q.wait()

    here = order_ref[ctx]
    there = [order_ref[other] for other in behind]
    span = 4 * rows
    factor = math.log2(math.e) / math.sqrt(HD)

    def attend(slot, late):
        slots = 8 if late else 4
        count = slots * rows
        queries = jnp.concatenate([q_buf[slot, :, h * HD : (h + 1) * HD] for h in range(group)], axis=0)
        key_rows = kv_buf[:, :slots, 0].reshape((PREV + 1) * count, HD)
        scores = lax.dot_general(
            queries, key_rows, (((1,), (1,)), ((), ())), preferred_element_type=jnp.float32
        )
        first = slot * rows - (span if late else 0)
        own_row = lax.broadcasted_iota(jnp.int32, (rows, span), 0) + first
        own_col = lax.broadcasted_iota(jnp.int32, (rows, span), 1)
        causal = jnp.where(own_col <= own_row, 0.0, MASKED_SCORE).astype(jnp.float32)
        causal = jnp.concatenate([causal] * group, axis=0)
        pieces = []
        for step in range(PREV + 1):
            for half in range(slots // 4):
                start = step * count + half * span
                piece = scores[:, start : start + span]
                if half == (1 if late else 0):
                    if step == 0:
                        piece = piece + causal
                    else:
                        seen = there[step - 1] > here if late else there[step - 1] < here
                        piece = piece + jnp.where(seen, 0.0, MASKED_SCORE).astype(jnp.float32)
                pieces.append(piece)
        top = functools.reduce(jnp.maximum, pieces)
        top = jnp.max(top, axis=1, keepdims=True)
        weights = jnp.concatenate([jnp.exp2((piece - top) * factor).astype(jnp.bfloat16) for piece in pieces], axis=1)
        total = jnp.dot(
            weights, vext[:, :count].reshape((PREV + 1) * count, 2 * HD), preferred_element_type=jnp.float32
        )
        result = (total[:, :HD] / total[:, HD:]).astype(jnp.bfloat16)
        for h in range(group):
            o_buf[slot, :, h * HD : (h + 1) * HD] = result[h * rows : (h + 1) * rows]

    own_out = pltpu.make_async_copy(o_buf.at[tp], out_hbm.at[:, lanes(tp, width)], local_sem.at[5])

    def serve(turn, carry):
        slot = slot_of(pick(turn, [dy for dy, _ in ORDER]), pick(turn, [dx for _, dx in ORDER]))

        @pl.when(turn > 0)
        def _():
            q_copy(slot, slot).wait_recv()

        @pl.when(slot < 4)
        def _():
            attend(slot, False)

        @pl.when(slot >= 4)
        def _():
            attend(slot, True)

        @pl.when(turn > 0)
        def _():
            o_copy(tp, slot).start()

        @pl.when(turn == 0)
        def _():
            own_out.start()

        return carry

    lax.fori_loop(0, len(ORDER), serve, 0)

    own_out.wait()
    for dy, dx in ORDER[1:]:
        slot = slot_of(dy, dx)
        o_copy(slot, slot).wait_recv()
    for dy, dx in ORDER[1:]:
        slot = slot_of(dy, dx)
        o_copy(tp, slot).wait_send()
        q_copy(tp, slot).wait_send()
        kv_copy(0, k_vm, tp, slot).wait_send()
        kv_copy(1, v_vm, tp, slot).wait_send()
    for slot in range(8):
        for step in range(1, PREV + 1):
            forward(slot, step).wait_send()


def per_device(queries, keys, values, block_order):
    rows, width = queries.shape
    part = width // 8
    any_space = pl.BlockSpec(memory_space=pl.ANY)
    return pl.pallas_call(
        functools.partial(kernel, block_order.shape[0]),
        out_shape=jax.ShapeDtypeStruct(queries.shape, jnp.bfloat16),
        in_specs=[any_space, any_space, any_space, pl.BlockSpec(memory_space=pltpu.SMEM)],
        out_specs=any_space,
        scratch_shapes=[
            pltpu.VMEM((8, rows, part), jnp.bfloat16),
            pltpu.VMEM((PREV + 1, 8, 2, rows, HD), jnp.bfloat16),
            pltpu.VMEM(keys.shape, jnp.bfloat16),
            pltpu.VMEM(values.shape, jnp.bfloat16),
            pltpu.VMEM((PREV + 1, 8 * rows, 2 * HD), jnp.bfloat16),
            pltpu.VMEM((8, rows, part), jnp.bfloat16),
            pltpu.SemaphoreType.DMA((6,)),
            pltpu.SemaphoreType.DMA((8, 2)),
            pltpu.SemaphoreType.DMA((8, 2)),
            pltpu.SemaphoreType.DMA((8,)),
            pltpu.SemaphoreType.DMA((8,)),
            pltpu.SemaphoreType.DMA((8, PREV)),
            pltpu.SemaphoreType.DMA((8, PREV)),
            pltpu.SemaphoreType.DMA((8,)),
            pltpu.SemaphoreType.DMA((8,)),
        ],
        compiler_params=pltpu.CompilerParams(
            collective_id=0, has_side_effects=True, vmem_limit_bytes=48 * 2**20
        ),
    )(queries, keys, values, block_order)


def solution(mesh):
    return jax.shard_map(
        per_device,
        mesh=mesh,
        in_specs=(P(("ctx", "tp"), None), P(("ctx", "tp"), None), P(("ctx", "tp"), None), P()),
        out_specs=P(("ctx", "tp"), None),
        check_vma=False,
    )
```

time: 92.2 us -> 49.4 us (0.54)
  the two profiles are of different devices: /device:TPU:2 before, /device:TPU:6 now
where the time goes in v1:
time: 49.4 us; the launch traced here: 49.1 us
  Pallas kernels  44.8 us (91%)
  local copies, waits for them, and re-layouts  4.35 us (9%)
    pallas_call x1, Pallas kernels, per_device(): pl.pallas_call(functools.partial(kernel, block_order.shape[0]), out_shape...  44.8 us
    unnamed x9, local copies, waits for them, and re-layouts  4.35 us

profile of v1, /device:TPU:6, one launch (start us, length us, event | category | flops | bytes accessed | tf_op | source)
XLA Modules:
  0.0 49.1 jit_solution(445914333479620606)
XLA Ops:
  0.0 0.0 copy-start
  0.0 1.1 %copy-done = bf16[32,12288]{1,0:T(8,128)(2,1)S(1)} copy-done((bf16[32,12288]{1,0:T(8,128)(2,1)S(1)}, bf16[32,12288]{1,0:T(8,128)(2,1)}, u32[]{:S(2)}) %copy-start) | copy-done | bytes 786456
  1.1 0.0 copy-start.1
  1.1 0.8 %copy-done.1 = bf16[32,1024]{1,0:T(8,128)(2,1)S(1)} copy-done((bf16[32,1024]{1,0:T(8,128)(2,1)S(1)}, bf16[32,1024]{1,0:T(8,128)(2,1)}, u32[]{:S(2)}) %copy-start.1) | copy-done | bytes 65560
  2.0 0.0 copy-start.2
  2.0 0.8 %copy-done.2 = bf16[32,1024]{1,0:T(8,128)(2,1)S(1)} copy-done((bf16[32,1024]{1,0:T(8,128)(2,1)S(1)}, bf16[32,1024]{1,0:T(8,128)(2,1)}, u32[]{:S(2)}) %copy-start.2) | copy-done | bytes 65560
  2.8 0.0 copy-start.3
  2.8 0.7 %copy-done.3 = s32[64]{0:T(128)S(1)} copy-done((s32[64]{0:T(128)S(1)}, s32[64]{0:T(128)}, u32[]{:S(2)}) %copy-start.3) | copy-done | bytes 280
  3.5 44.8 %shard_map.46 = bf16[32,12288]{1,0:T(8,128)(2,1)S(1)} custom-call(bf16[32,12288]{1,0:T(8,128)(2,1)S(1)} %copy-done, bf16[32,1024]{1,0:T(8,128)(2,1)S(1)} %copy-done.1, bf16[32,1024]{1,0:T(8,128)(2,1)S(1)} %copy-done.2, s32[64]{0:T(128)S(1)} %copy-done.3), custom_call_target="tpu_custom_call" | custom-call | tf_op jit(solution)/shard_map/pallas_call | solution.py:216
  48.2 0.9 %copy.6 = bf16[32,12288]{1,0:T(8,128)(2,1)} copy(bf16[32,12288]{1,0:T(8,128)(2,1)S(1)} %shard_map.46) | data formatting | bytes 1572864
Async XLA Ops:
  0.0 1.1 %copy-start = (bf16[32,12288]{1,0:T(8,128)(2,1)S(1)}, bf16[32,12288]{1,0:T(8,128)(2,1)}, u32[]{:S(2)}) copy-start(bf16[32,12288]{1,0:T(8,128)(2,1)} %q_hbm.1) | copy-start | bytes 2359300
  1.1 0.8 %copy-start.1 = (bf16[32,1024]{1,0:T(8,128)(2,1)S(1)}, bf16[32,1024]{1,0:T(8,128)(2,1)}, u32[]{:S(2)}) copy-start(bf16[32,1024]{1,0:T(8,128)(2,1)} %k_hbm.1) | copy-start | bytes 196612
  2.0 0.8 %copy-start.2 = (bf16[32,1024]{1,0:T(8,128)(2,1)S(1)}, bf16[32,1024]{1,0:T(8,128)(2,1)}, u32[]{:S(2)}) copy-start(bf16[32,1024]{1,0:T(8,128)(2,1)} %v_hbm.1) | copy-start | bytes 196612
  2.8 0.7 %copy-start.3 = (s32[64]{0:T(128)S(1)}, s32[64]{0:T(128)}, u32[]{:S(2)}) copy-start(s32[64]{0:T(128)} %order_ref.1) | copy-start | bytes 772

commit v2 on v1

v2 whole, which is shorter than its diff:
```python
import functools
import math

import jax
import jax.numpy as jnp
from jax import lax
from jax.experimental import pallas as pl
from jax.experimental.pallas import tpu as pltpu
from jax.sharding import PartitionSpec as P

HD = 128
PREV = 3
MASKED_SCORE = -1e30
MESH = pl.DeviceIdType.MESH
ORDER = ((2, 1), (1, 1), (3, 1), (2, 0), (0, 1), (1, 0), (3, 0), (0, 0))
PEERS = ORDER[:-1]


def pick(index, values):
    total = jnp.int32(0)
    for position, value in enumerate(values):
        if value:
            total = total + jnp.where(index == position, jnp.int32(value), jnp.int32(0))
    return total


def kernel(
    blocks, q_hbm, k_hbm, v_hbm, order_hbm, out_ref,
    order_ref, q_buf, kv_buf, kv_own, vext, o_buf,
    order_sem, own_sem, load_sem, q_own_sem, o_own_sem,
    s_ss, s_rs, r_ss, q_ss, q_rs, o_ss, o_rs,
):
    ctx = lax.axis_index("ctx")
    tp = lax.axis_index("tp")
    planes = blocks // 2
    rows = q_hbm.shape[0]
    width = q_buf.shape[2]
    group = width // HD
    w, c = lax.div(ctx, 2), lax.rem(ctx, 2)
    y, xh = lax.div(tp, 2), lax.rem(tp, 2)

    def near(dy, dx):
        return lax.rem(y + dy, 4) * 2 + lax.rem(xh + dx, 2)

    def block_at(dw, core):
        return lax.rem(w + dw + planes, planes) * 2 + core

    def lanes(index, size):
        return pl.ds(pl.multiple_of(index * size, size), size)

    mate = (block_at(0, 1 - c), tp)

    loads = []
    for part, source in enumerate((k_hbm, v_hbm)):
        for h in range(8):
            loads.append(
                pltpu.make_async_copy(source.at[:, pl.ds(h * HD, HD)], kv_own.at[h, part], load_sem.at[h, part])
            )
    own_kv = [
        pltpu.make_async_copy(source.at[:, lanes(tp, HD)], kv_buf.at[0, tp, part], own_sem.at[part])
        for part, source in enumerate((k_hbm, v_hbm))
    ]
    own_q = pltpu.make_async_copy(q_hbm.at[:, lanes(tp, width)], q_buf.at[tp], q_own_sem)
    order_load = pltpu.make_async_copy(order_hbm, order_ref, order_sem)
    for copy in (*loads, *own_kv, own_q, order_load):
        copy.start()

    barrier = pltpu.get_barrier_semaphore()

    def greet(block, slot):
        pl.semaphore_signal(barrier, inc=1, device_id=(block, slot), device_id_type=MESH)

    for dy, dx in ORDER:
        greet(block_at(-1, c), near(dy, dx))

    @pl.when(c == 0)
    def _():
        for dy, dx in ORDER:
            greet(block_at(-2, 1), near(dy, dx))

    for dy, dx in PEERS:
        greet(ctx, near(dy, dx))
    greet(*mate)
    pl.semaphore_wait(barrier, 16 + 8 * c)

    def slice_copy(dw, slot):
        return pltpu.make_async_remote_copy(
            src_ref=kv_own.at[slot],
            dst_ref=kv_buf.at[(0, 2, 3)[dw], tp],
            send_sem=s_ss.at[dw, slot],
            recv_sem=s_rs.at[(0, 2, 3)[dw], tp],
            device_id=(block_at(dw, 0 if dw == 2 else c), slot),
            device_id_type=MESH,
        )

    def relay(offset, landing, slot):
        return pltpu.make_async_remote_copy(
            src_ref=kv_buf.at[offset, slot],
            dst_ref=kv_buf.at[landing, slot],
            send_sem=r_ss.at[offset // 2, slot],
            recv_sem=s_rs.at[landing, slot],
            device_id=mate,
            device_id_type=MESH,
        )

    def arrived(offset, slot):
        relay(0, offset, slot).wait_recv()

    def q_copy(origin, slot):
        return pltpu.make_async_remote_copy(
            src_ref=q_hbm.at[:, lanes(slot, width)],
            dst_ref=q_buf.at[origin],
            send_sem=q_ss.at[slot],
            recv_sem=q_rs.at[origin],
            device_id=(ctx, slot),
            device_id_type=MESH,
        )

    def o_copy(origin, slot):
        return pltpu.make_async_remote_copy(
            src_ref=o_buf.at[slot],
            dst_ref=out_ref.at[:, lanes(origin, width)],
            send_sem=o_ss.at[slot],
            recv_sem=o_rs.at[origin],
            device_id=(ctx, slot),
            device_id_type=MESH,
        )

    for copy in loads:
        copy.wait()
    for dy, dx in ORDER:
        slice_copy(1, near(dy, dx)).start()

    @pl.when(c == 1)
    def _():
        for dy, dx in ORDER:
            slice_copy(2, near(dy, dx)).start()

    for dy, dx in PEERS:
        slice_copy(0, near(dy, dx)).start()
    for dy, dx in PEERS:
        q_copy(tp, near(dy, dx)).start()

    for copy in own_kv:
        copy.wait()
    for dy, dx in reversed(PEERS):
        arrived(0, near(dy, dx))

        @pl.when(c == 0)
        def _(slot=near(dy, dx)):
            relay(0, 1, slot).start()

    @pl.when(c == 0)
    def _():
        relay(0, 1, tp).start()

    for dy, dx in reversed(ORDER):
        arrived(2, near(dy, dx))

        @pl.when(c == 0)
        def _(slot=near(dy, dx)):
            relay(2, 3, slot).start()

        @pl.when(c == 1)
        def _(slot=near(dy, dx)):
            relay(2, 1, slot).start()

    vext[:, :, HD:] = jnp.ones((PREV + 1, 8 * rows, HD), jnp.bfloat16)
    for offset in (0, 2, 1, 3):
        if offset % 2:
            for slot in range(8):
                arrived(offset, slot)
        vext[offset, :, :HD] = kv_buf[offset, :, 1].reshape(8 * rows, HD)
    own_q.wait()
    order_load.wait()

    span = 4 * rows
    factor = math.log2(math.e) / math.sqrt(HD)

    here = order_ref[ctx]
    there = [order_ref[lax.rem(ctx + blocks - step, blocks)] for step in range(1, PREV + 1)]

    def attend(slot, late):
        slots = 8 if late else 4
        count = slots * rows
        queries = jnp.concatenate([q_buf[slot, :, h * HD : (h + 1) * HD] for h in range(group)], axis=0)
        key_rows = kv_buf[:, :slots, 0].reshape((PREV + 1) * count, HD)
        scores = lax.dot_general(
            queries, key_rows, (((1,), (1,)), ((), ())), preferred_element_type=jnp.float32
        )
        first = slot * rows - (span if late else 0)
        own_row = lax.broadcasted_iota(jnp.int32, (rows, span), 0) + first
        own_col = lax.broadcasted_iota(jnp.int32, (rows, span), 1)
        causal = jnp.where(own_col <= own_row, 0.0, MASKED_SCORE).astype(jnp.float32)
        causal = jnp.concatenate([causal] * group, axis=0)
        pieces = []
        for step in range(PREV + 1):
            for half in range(count // span):
                start = step * count + half * span
                piece = scores[:, start : start + span]
                if half == (1 if late else 0):
                    if step == 0:
                        piece = piece + causal
                    else:
                        seen = there[step - 1] > here if late else there[step - 1] < here
                        piece = piece + jnp.where(seen, 0.0, MASKED_SCORE).astype(jnp.float32)
                pieces.append(piece)
        top = functools.reduce(jnp.maximum, pieces)
        top = jnp.max(top, axis=1, keepdims=True)
        weights = jnp.concatenate([jnp.exp2((piece - top) * factor).astype(jnp.bfloat16) for piece in pieces], axis=1)
        total = jnp.dot(
            weights, vext[:, :count].reshape((PREV + 1) * count, 2 * HD), preferred_element_type=jnp.float32
        )
        result = (total[:, :HD] / total[:, HD:]).astype(jnp.bfloat16)
        for h in range(group):
            o_buf[slot, :, h * HD : (h + 1) * HD] = result[h * rows : (h + 1) * rows]

    own_out = pltpu.make_async_copy(o_buf.at[tp], out_ref.at[:, lanes(tp, width)], o_own_sem)

    def serve(turn, carry):
        slot = near(pick(turn, [dy for dy, _ in ORDER]), pick(turn, [dx for _, dx in ORDER]))

        @pl.when(turn < len(PEERS))
        def _():
            q_copy(slot, slot).wait_recv()

        @pl.when(slot < 4)
        def _():
            attend(slot, False)

        @pl.when(slot >= 4)
        def _():
            attend(slot, True)

        @pl.when(turn < len(PEERS))
        def _():
            o_copy(tp, slot).start()

        return carry

    lax.fori_loop(0, len(ORDER), serve, 0)
    own_out.start()

    for dy, dx in PEERS:
        slot = near(dy, dx)
        q_copy(tp, slot).wait_send()
        slice_copy(0, slot).wait_send()
    for dy, dx in ORDER:
        slot = near(dy, dx)
        slice_copy(1, slot).wait_send()
        relay(2, 1, slot).wait_send()

    @pl.when(c == 0)
    def _():
        for dy, dx in ORDER:
            relay(0, 1, near(dy, dx)).wait_send()

    @pl.when(c == 1)
    def _():
        for dy, dx in ORDER:
            slice_copy(2, near(dy, dx)).wait_send()

    own_out.wait()
    for dy, dx in PEERS:
        slot = near(dy, dx)
        o_copy(tp, slot).wait_send()
        o_copy(slot, slot).wait_recv()


def per_device(queries, keys, values, block_order):
    rows, width = queries.shape
    part = width // 8
    hbm = pl.BlockSpec(memory_space=pl.ANY)
    window = PREV + 1
    dma = pltpu.SemaphoreType.DMA
    return pl.pallas_call(
        functools.partial(kernel, block_order.shape[0]),
        out_shape=jax.ShapeDtypeStruct(queries.shape, jnp.bfloat16),
        in_specs=[hbm, hbm, hbm, hbm],
        out_specs=hbm,
        scratch_shapes=[
            pltpu.SMEM(block_order.shape, jnp.int32),
            pltpu.VMEM((8, rows, part), jnp.bfloat16),
            pltpu.VMEM((window, 8, 2, rows, HD), jnp.bfloat16),
            pltpu.VMEM((8, 2, rows, HD), jnp.bfloat16),
            pltpu.VMEM((window, 8 * rows, 2 * HD), jnp.bfloat16),
            pltpu.VMEM((8, rows, part), jnp.bfloat16),
            dma, dma((2,)), dma((8, 2)), dma, dma,
            dma((3, 8)), dma((window, 8)), dma((2, 8)),
            dma((8,)), dma((8,)), dma((8,)), dma((8,)),
        ],
        compiler_params=pltpu.CompilerParams(
            collective_id=0, has_side_effects=True, vmem_limit_bytes=65500000
        ),
    )(queries, keys, values, block_order)


def solution(mesh):
    return jax.shard_map(
        per_device,
        mesh=mesh,
        in_specs=(P(("ctx", "tp"), None), P(("ctx", "tp"), None), P(("ctx", "tp"), None), P()),
        out_specs=P(("ctx", "tp"), None),
        check_vma=False,
    )
```

time: 49.4 us -> 40.6 us (0.82)
  the two profiles are of different devices: /device:TPU:6 before, /device:TPU:1 now
where the time goes in v2:
time: 40.6 us; the launch traced here: 40.5 us
  Pallas kernels  38.4 us (95%)
  local copies, waits for them, and re-layouts  2.06 us (5%)
    pallas_call x1, Pallas kernels, per_device(): pl.pallas_call(functools.partial(kernel, block_order.shape[0]), out_shape...  38.4 us
    unnamed x1, local copies, waits for them, and re-layouts  2.06 us

profile of v2, /device:TPU:1, one launch (start us, length us, event | category | flops | bytes accessed | tf_op | source)
XLA Modules:
  0.0 40.5 jit_solution(7698279802893869967)
XLA Ops:
  0.0 38.4 %shard_map.46 = bf16[32,12288]{1,0:T(8,128)(2,1)} custom-call(bf16[32,12288]{1,0:T(8,128)(2,1)} %q_hbm.1, bf16[32,1024]{1,0:T(8,128)(2,1)} %k_hbm.1, bf16[32,1024]{1,0:T(8,128)(2,1)} %v_hbm.1, s32[64]{0:T(128)} %order_hbm.1), custom_call_target="tpu_custom_call" | custom-call | tf_op jit(solution)/shard_map/pallas_call | solution.py:276
  38.4 2.1 %copy.6 = bf16[32,12288]{1,0:T(8,128)(2,1)} copy(bf16[32,12288]{1,0:T(8,128)(2,1)} %shard_map.46) | data formatting | bytes 1572864

commit v3 on v2

--- a/solution.py
+++ b/solution.py
@@ -75,21 +75,30 @@
 
     @pl.when(c == 0)
     def _():
-        for dy, dx in ORDER:
-            greet(block_at(-2, 1), near(dy, dx))
+        greet(block_at(-1, 1), tp)
 
     for dy, dx in PEERS:
         greet(ctx, near(dy, dx))
     greet(*mate)
-    pl.semaphore_wait(barrier, 16 + 8 * c)
+    pl.semaphore_wait(barrier, 16 + c)
 
     def slice_copy(dw, slot):
         return pltpu.make_async_remote_copy(
             src_ref=kv_own.at[slot],
-            dst_ref=kv_buf.at[(0, 2, 3)[dw], tp],
+            dst_ref=kv_buf.at[2 * dw, tp],
             send_sem=s_ss.at[dw, slot],
-            recv_sem=s_rs.at[(0, 2, 3)[dw], tp],
-            device_id=(block_at(dw, 0 if dw == 2 else c), slot),
+            recv_sem=s_rs.at[2 * dw, tp],
+            device_id=(block_at(dw, c), slot),
+            device_id_type=MESH,
+        )
+
+    def onward(slot):
+        return pltpu.make_async_remote_copy(
+            src_ref=kv_buf.at[2, slot],
+            dst_ref=kv_buf.at[3, slot],
+            send_sem=s_ss.at[2, slot],
+            recv_sem=s_rs.at[3, slot],
+            device_id=(block_at(1, 0), tp),
             device_id_type=MESH,
         )
 
@@ -131,11 +140,6 @@
     for dy, dx in ORDER:
         slice_copy(1, near(dy, dx)).start()
 
-    @pl.when(c == 1)
-    def _():
-        for dy, dx in ORDER:
-            slice_copy(2, near(dy, dx)).start()
-
     for dy, dx in PEERS:
         slice_copy(0, near(dy, dx)).start()
     for dy, dx in PEERS:
@@ -163,6 +167,7 @@
 
         @pl.when(c == 1)
         def _(slot=near(dy, dx)):
+            onward(slot).start()
             relay(2, 1, slot).start()
 
     vext[:, :, HD:] = jnp.ones((PREV + 1, 8 * rows, HD), jnp.bfloat16)
@@ -258,7 +263,7 @@
     @pl.when(c == 1)
     def _():
         for dy, dx in ORDER:
-            slice_copy(2, near(dy, dx)).wait_send()
+            onward(near(dy, dx)).wait_send()
 
     own_out.wait()
     for dy, dx in PEERS:
@@ -290,9 +295,9 @@
             dma((8,)), dma((8,)), dma((8,)), dma((8,)),
         ],
         compiler_params=pltpu.CompilerParams(
-            collective_id=0, has_side_effects=True, vmem_limit_bytes=65500000
+            collective_id=0, has_side_effects=True, vmem_limit_bytes=50331648
         ),
-    )(queries, keys, values, block_order)
+    )(*[pltpu.with_memory_space_constraint(a, pltpu.HBM) for a in (queries, keys, values, block_order)])
 
 
 def solution(mesh):

time: 40.6 us -> 37.8 us (0.931)
  Pallas kernels: 38.4 us -> 36.8 us
  local copies, waits for them, and re-layouts: 2.06 us -> 0.88 us
    pallas_call x1, Pallas kernels: 38.4 us -> 36.8 us  [per_device(): pl.pallas_call(functools.partial(kernel, block_order.shape[0]), out_shape...]
    unnamed x1, local copies, waits for them, and re-layouts: 2.06 us -> 0.88 us
where the time goes in v3:
time: 37.8 us; the launch traced here: 37.7 us
  Pallas kernels  36.8 us (97%)
  local copies, waits for them, and re-layouts  0.88 us (2%)
    pallas_call x1, Pallas kernels, per_device(): pl.pallas_call(functools.partial(kernel, block_order.shape[0]), out_shape...  36.8 us
    unnamed x1, local copies, waits for them, and re-layouts  0.88 us

profile of v3, /device:TPU:1, one launch (start us, length us, event | category | flops | bytes accessed | tf_op | source)
XLA Modules:
  0.0 37.7 jit_solution(9594374404500990115)
XLA Ops:
  0.0 36.8 %shard_map.46 = bf16[32,12288]{1,0:T(8,128)(2,1)S(1)} custom-call(bf16[32,12288]{1,0:T(8,128)(2,1)} %q_hbm.1, bf16[32,1024]{1,0:T(8,128)(2,1)} %k_hbm.1, bf16[32,1024]{1,0:T(8,128)(2,1)} %v_hbm.1, s32[64]{0:T(128)} %order_hbm.1), custom_call_target="tpu_custom_call" | custom-call | tf_op jit(solution)/shard_map/pallas_call | solution.py:281
  36.8 0.9 %copy.6 = bf16[32,12288]{1,0:T(8,128)(2,1)} copy(bf16[32,12288]{1,0:T(8,128)(2,1)S(1)} %shard_map.46) | data formatting | bytes 1572864

commit v4 on v3

--- a/solution.py
+++ b/solution.py
@@ -14,6 +14,7 @@
 MESH = pl.DeviceIdType.MESH
 ORDER = ((2, 1), (1, 1), (3, 1), (2, 0), (0, 1), (1, 0), (3, 0), (0, 0))
 PEERS = ORDER[:-1]
+PARTS = ((0, 1), (2, 3))
 
 
 def pick(index, values):
@@ -27,7 +28,7 @@
 def kernel(
     blocks, q_hbm, k_hbm, v_hbm, order_hbm, out_ref,
     order_ref, q_buf, kv_buf, kv_own, vext, o_buf,
-    order_sem, own_sem, load_sem, q_own_sem, o_own_sem,
+    clear_sem, order_sem, own_sem, load_sem, q_own_sem, o_own_sem,
     s_ss, s_rs, r_ss, q_ss, q_rs, o_ss, o_rs,
 ):
     ctx = lax.axis_index("ctx")
@@ -77,10 +78,19 @@
     def _():
         greet(block_at(-1, 1), tp)
 
-    for dy, dx in PEERS:
-        greet(ctx, near(dy, dx))
+    last = lax.rem(w, planes // 2) == planes // 2 - 1
+
+    @pl.when(jnp.logical_not(last))
+    def _():
+        for dy, dx in PEERS:
+            greet(ctx, near(dy, dx))
+
     greet(*mate)
-    pl.semaphore_wait(barrier, 16 + c)
+    pl.semaphore_wait(barrier, jnp.where(last, 9 + c, 16 + c))
+
+    @pl.when(lax.rem(w + 1, planes // 2) == planes // 2 - 1)
+    def _():
+        pl.semaphore_signal(clear_sem, inc=1, device_id=(block_at(1, c), tp), device_id_type=MESH)
 
     def slice_copy(dw, slot):
         return pltpu.make_async_remote_copy(
@@ -139,6 +149,10 @@
         copy.wait()
     for dy, dx in ORDER:
         slice_copy(1, near(dy, dx)).start()
+
+    @pl.when(last)
+    def _():
+        pl.semaphore_wait(clear_sem, 1)
 
     for dy, dx in PEERS:
         slice_copy(0, near(dy, dx)).start()
@@ -189,33 +203,47 @@
         slots = 8 if late else 4
         count = slots * rows
         queries = jnp.concatenate([q_buf[slot, :, h * HD : (h + 1) * HD] for h in range(group)], axis=0)
-        key_rows = kv_buf[:, :slots, 0].reshape((PREV + 1) * count, HD)
-        scores = lax.dot_general(
-            queries, key_rows, (((1,), (1,)), ((), ())), preferred_element_type=jnp.float32
-        )
         first = slot * rows - (span if late else 0)
         own_row = lax.broadcasted_iota(jnp.int32, (rows, span), 0) + first
         own_col = lax.broadcasted_iota(jnp.int32, (rows, span), 1)
         causal = jnp.where(own_col <= own_row, 0.0, MASKED_SCORE).astype(jnp.float32)
         causal = jnp.concatenate([causal] * group, axis=0)
-        pieces = []
-        for step in range(PREV + 1):
-            for half in range(count // span):
-                start = step * count + half * span
-                piece = scores[:, start : start + span]
-                if half == (1 if late else 0):
-                    if step == 0:
-                        piece = piece + causal
-                    else:
-                        seen = there[step - 1] > here if late else there[step - 1] < here
-                        piece = piece + jnp.where(seen, 0.0, MASKED_SCORE).astype(jnp.float32)
-                pieces.append(piece)
-        top = functools.reduce(jnp.maximum, pieces)
-        top = jnp.max(top, axis=1, keepdims=True)
-        weights = jnp.concatenate([jnp.exp2((piece - top) * factor).astype(jnp.bfloat16) for piece in pieces], axis=1)
-        total = jnp.dot(
-            weights, vext[:, :count].reshape((PREV + 1) * count, 2 * HD), preferred_element_type=jnp.float32
-        )
+
+        def scored(offsets):
+            key_rows = kv_buf[offsets[0] : offsets[-1] + 1, :slots, 0].reshape(len(offsets) * count, HD)
+            scores = lax.dot_general(
+                queries, key_rows, (((1,), (1,)), ((), ())), preferred_element_type=jnp.float32
+            )
+            pieces = []
+            for position, offset in enumerate(offsets):
+                for half in range(slots // 4):
+                    start = position * count + half * span
+                    piece = scores[:, start : start + span]
+                    if half == (1 if late else 0):
+                        if offset == 0:
+                            piece = piece + causal
+                        else:
+                            seen = there[offset - 1] > here if late else there[offset - 1] < here
+                            piece = piece + jnp.where(seen, 0.0, MASKED_SCORE).astype(jnp.float32)
+                    pieces.append(piece)
+            return pieces
+
+        total, top = None, None
+        parts = [scored(offsets) for offsets in PARTS]
+        for offsets, pieces in zip(PARTS, parts):
+            best = jnp.max(functools.reduce(jnp.maximum, pieces), axis=1, keepdims=True)
+            if top is not None:
+                best = jnp.maximum(best, top)
+            weights = jnp.concatenate(
+                [jnp.exp2((piece - best) * factor).astype(jnp.bfloat16) for piece in pieces], axis=1
+            )
+            sums = jnp.dot(
+                weights,
+                vext[offsets[0] : offsets[-1] + 1, :count].reshape(len(offsets) * count, 2 * HD),
+                preferred_element_type=jnp.float32,
+            )
+            total = sums if total is None else total * jnp.exp2((top - best) * factor) + sums
+            top = best
         result = (total[:, :HD] / total[:, HD:]).astype(jnp.bfloat16)
         for h in range(group):
             o_buf[slot, :, h * HD : (h + 1) * HD] = result[h * rows : (h + 1) * rows]
@@ -290,7 +318,7 @@
             pltpu.VMEM((8, 2, rows, HD), jnp.bfloat16),
             pltpu.VMEM((window, 8 * rows, 2 * HD), jnp.bfloat16),
             pltpu.VMEM((8, rows, part), jnp.bfloat16),
-            dma, dma((2,)), dma((8, 2)), dma, dma,
+            pltpu.SemaphoreType.REGULAR, dma, dma((2,)), dma((8, 2)), dma, dma,
             dma((3, 8)), dma((window, 8)), dma((2, 8)),
             dma((8,)), dma((8,)), dma((8,)), dma((8,)),
         ],

time: 37.8 us -> 34.8 us (0.921)
  the two profiles are of different devices: /device:TPU:1 before, /device:TPU:8 now
where the time goes in v4:
time: 34.8 us; the launch traced here: 34.7 us
  Pallas kernels  33.8 us (97%)
  local copies, waits for them, and re-layouts  0.88 us (3%)
    pallas_call x1, Pallas kernels, per_device(): pl.pallas_call(functools.partial(kernel, block_order.shape[0]), out_shape...  33.8 us
    unnamed x1, local copies, waits for them, and re-layouts  0.88 us

profile of v4, /device:TPU:8, one launch (start us, length us, event | category | flops | bytes accessed | tf_op | source)
XLA Modules:
  0.0 34.7 jit_solution(2815901202800878450)
XLA Ops:
  0.0 33.8 %shard_map.46 = bf16[32,12288]{1,0:T(8,128)(2,1)S(1)} custom-call(bf16[32,12288]{1,0:T(8,128)(2,1)} %q_hbm.1, bf16[32,1024]{1,0:T(8,128)(2,1)} %k_hbm.1, bf16[32,1024]{1,0:T(8,128)(2,1)} %v_hbm.1, s32[64]{0:T(128)} %order_hbm.1), custom_call_target="tpu_custom_call" | custom-call | tf_op jit(solution)/shard_map/pallas_call | solution.py:309
  33.8 0.9 %copy.6 = bf16[32,12288]{1,0:T(8,128)(2,1)} copy(bf16[32,12288]{1,0:T(8,128)(2,1)S(1)} %shard_map.46) | data formatting | bytes 1572864

commit v5 on v4

--- a/solution.py
+++ b/solution.py
@@ -12,7 +12,7 @@
 PREV = 3
 MASKED_SCORE = -1e30
 MESH = pl.DeviceIdType.MESH
-ORDER = ((2, 1), (1, 1), (3, 1), (2, 0), (0, 1), (1, 0), (3, 0), (0, 0))
+ORDER = ((2, 1), (1, 0), (1, 1), (3, 0), (3, 1), (2, 0), (0, 1), (0, 0))
 PEERS = ORDER[:-1]
 PARTS = ((0, 1), (2, 3))
 

time: 34.8 us -> 34.9 us (level)
  no operation moved by 1% of the time
where the time goes in v5:
time: 34.9 us; the launch traced here: 34.8 us
  Pallas kernels  33.9 us (97%)
  local copies, waits for them, and re-layouts  0.88 us (3%)
    pallas_call x1, Pallas kernels, per_device(): pl.pallas_call(functools.partial(kernel, block_order.shape[0]), out_shape...  33.9 us
    unnamed x1, local copies, waits for them, and re-layouts  0.88 us

profile of v5, /device:TPU:8, one launch (start us, length us, event | category | flops | bytes accessed | tf_op | source)
XLA Modules:
  0.0 34.8 jit_solution(6581598223659262278)
XLA Ops:
  0.0 33.9 %shard_map.46 = bf16[32,12288]{1,0:T(8,128)(2,1)S(1)} custom-call(bf16[32,12288]{1,0:T(8,128)(2,1)} %q_hbm.1, bf16[32,1024]{1,0:T(8,128)(2,1)} %k_hbm.1, bf16[32,1024]{1,0:T(8,128)(2,1)} %v_hbm.1, s32[64]{0:T(128)} %order_hbm.1), custom_call_target="tpu_custom_call" | custom-call | tf_op jit(solution)/shard_map/pallas_call | solution.py:309
  33.9 0.9 %copy.6 = bf16[32,12288]{1,0:T(8,128)(2,1)} copy(bf16[32,12288]{1,0:T(8,128)(2,1)S(1)} %shard_map.46) | data formatting | bytes 1572864

commit v6 on v4

--- a/solution.py
+++ b/solution.py
@@ -63,7 +63,7 @@
     ]
     own_q = pltpu.make_async_copy(q_hbm.at[:, lanes(tp, width)], q_buf.at[tp], q_own_sem)
     order_load = pltpu.make_async_copy(order_hbm, order_ref, order_sem)
-    for copy in (*loads, *own_kv, own_q, order_load):
+    for copy in loads:
         copy.start()
 
     barrier = pltpu.get_barrier_semaphore()
@@ -86,6 +86,8 @@
             greet(ctx, near(dy, dx))
 
     greet(*mate)
+    for copy in (*own_kv, own_q, order_load):
+        copy.start()
     pl.semaphore_wait(barrier, jnp.where(last, 9 + c, 16 + c))
 
     @pl.when(lax.rem(w + 1, planes // 2) == planes // 2 - 1)

time: 34.8 us -> 34.8 us (level)
  no operation moved by 1% of the time
where the time goes in v6:
time: 34.8 us; the launch traced here: 34.7 us
  Pallas kernels  33.8 us (97%)
  local copies, waits for them, and re-layouts  0.88 us (3%)
    pallas_call x1, Pallas kernels, per_device(): pl.pallas_call(functools.partial(kernel, block_order.shape[0]), out_shape...  33.8 us
    unnamed x1, local copies, waits for them, and re-layouts  0.88 us

profile of v6, /device:TPU:8, one launch (start us, length us, event | category | flops | bytes accessed | tf_op | source)
XLA Modules:
  0.0 34.7 jit_solution(3334008688460501162)
XLA Ops:
  0.0 33.8 %shard_map.46 = bf16[32,12288]{1,0:T(8,128)(2,1)S(1)} custom-call(bf16[32,12288]{1,0:T(8,128)(2,1)} %q_hbm.1, bf16[32,1024]{1,0:T(8,128)(2,1)} %k_hbm.1, bf16[32,1024]{1,0:T(8,128)(2,1)} %v_hbm.1, s32[64]{0:T(128)} %order_hbm.1), custom_call_target="tpu_custom_call" | custom-call | tf_op jit(solution)/shard_map/pallas_call | solution.py:311
  33.8 0.9 %copy.6 = bf16[32,12288]{1,0:T(8,128)(2,1)} copy(bf16[32,12288]{1,0:T(8,128)(2,1)S(1)} %shard_map.46) | data formatting | bytes 1572864
